TPU v7x, 256 devices: a whole 4x4x8 slice. The times are simulated.
256 devices in a mesh: rep: 2 (over core), dp: 128 (over x, y, z).
Axes of the slice: x: 4, y: 4, z: 8, core: 2. Of those that a mesh axis runs over, the one named last changes fastest.
Arguments:
- g_w_gate: bfloat16 [256, 2, 896, 2304], P(('rep', 'dp')), parts along dimension 0
- g_w_up: bfloat16 [256, 2, 896, 2304], P(('rep', 'dp')), parts along dimension 0
- g_w_down: bfloat16 [256, 2, 2304, 896], P(('rep', 'dp')), parts along dimension 0
- w_gate: bfloat16 [2, 896, 2304], replicated
- w_up: bfloat16 [2, 896, 2304], replicated
- w_down: bfloat16 [2, 2304, 896], replicated
- m_w_gate: float32 [2, 896, 2304], P(None, 'dp')
- m_w_up: float32 [2, 896, 2304], P(None, 'dp')
- m_w_down: float32 [2, 2304, 896], P(None, 'dp')
- v_w_gate: float32 [2, 896, 2304], P(None, 'dp')
- v_w_up: float32 [2, 896, 2304], P(None, 'dp')
- v_w_down: float32 [2, 2304, 896], P(None, 'dp')
Outputs:
- output 1: bfloat16 [4, 896, 2304], P('rep'), parts along dimension 0
- output 2: bfloat16 [4, 896, 2304], P('rep'), parts along dimension 0
- output 3: bfloat16 [4, 2304, 896], P('rep'), parts along dimension 0
- output 4: float32 [4, 896, 2304], P('rep', 'dp'), parts along dimension 0
- output 5: float32 [4, 896, 2304], P('rep', 'dp'), parts along dimension 0
- output 6: float32 [4, 2304, 896], P('rep', 'dp'), parts along dimension 0
- output 7: float32 [4, 896, 2304], P('rep', 'dp'), parts along dimension 0
- output 8: float32 [4, 896, 2304], P('rep', 'dp'), parts along dimension 0
- output 9: float32 [4, 2304, 896], P('rep', 'dp'), parts along dimension 0
There are 2 independent parts. A program takes and returns all parts, laid end to end along the dimension named above; an argument that names none is the same for every part.
All inputs are finite; a program needn't handle non-finite values.
Results may differ from a plain program's by a relative error of at most 0.022.
Values are sent between devices in bfloat16 or wider.
A program may use at most 768 MiB of HBM per device.

v0:
```python
import jax
import jax.numpy as jnp
from jax import lax
from jax.sharding import PartitionSpec as P


def adamw(w, m, v, g):
    m = 0.9 * m + 0.1 * g
    v = 0.95 * v + 0.05 * g * g
    step = m * lax.rsqrt(v + 1e-8) + 0.1 * w
    return (w - 0.02 * step).astype(jnp.bfloat16), m, v


def solution(mesh):
    def step(*arrays):
        terms, weights, m, v = (arrays[i : i + 3] for i in (0, 3, 6, 9))
        gradients = [lax.psum_scatter(t[0], "dp", scatter_dimension=1, tiled=True).astype(jnp.float32) for t in terms]
        me = lax.axis_index("dp")
        own = [lax.dynamic_slice_in_dim(w, me * one.shape[1], one.shape[1], 1).astype(jnp.float32) for w, one in zip(weights, m, strict=True)]
        new = [adamw(w, m, v, g) for w, m, v, g in zip(own, m, v, gradients, strict=True)]
        whole = [lax.all_gather(one[0], "dp", axis=1, tiled=True) for one in new]
        return (*whole, *(one[1] for one in new), *(one[2] for one in new))

    all_of, cut = P(None, None, None), P(None, "dp", None)
    return jax.shard_map(
        step,
        mesh=mesh,
        in_specs=(P(("rep", "dp"), None, None, None),) * 3 + (all_of,) * 3 + (cut,) * 6,
        out_specs=(P("rep", None, None),) * 3 + (P("rep", "dp", None),) * 6,
        check_vma=False,
    )
```

profile of v0, /device:TPU:32, one launch (start us, length us, event | category | flops | bytes accessed | tf_op | source)
XLA Modules:
  0.0 902.5 jit_solution(5258868353873410610)
XLA Ops:
  7.2 0.0 all-reduce.6.cloned.1.call-start
  7.2 36.7 %copy.48 = bf16[1,2,2304,896]{3,1,2,0:T(2,128)(2,1)} copy(bf16[1,2,2304,896]{3,2,1,0:T(8,128)(2,1)} %param.14) | data formatting | bytes 16515072 | tf_op args[2]
  44.0 41.9 %copy_bitcast_fusion.1 = (bf16[2,896,2304]{2,0,1:T(2,128)(2,1)}, bf16[2,896,2304]{2,0,1:T(2,128)(2,1)}) fusion(bf16[1,2,896,2304]{3,2,1,0:T(8,128)(2,1)S(1)} %copy-done, bf16[1,2,896,2304]{3,2,1,0:T(8,128)(2,1)S(1)} %copy-done.1), kind=kLoop, calls=%fused_computation.1 | loop fusion | bytes 33030144 | tf_op jit(solution)/shard_map/squeeze | solution.py:17
  86.0 0.0 all-reduce.6.cloned.1.call-update
  86.0 0.0 all-gather.6.cloned.1.call-start
  86.1 0.5 copy-done.8
  86.6 0.6 dynamic-slice
  87.9 1.0 constant_dynamic-slice_fusion.1
  88.9 423.7 %all-reduce.6.cloned.1.call-done = (bf16[2,896,2304]{2,0,1:T(2,128)(2,1)}, bf16[2,896,2304]{2,0,1:T(2,128)(2,1)}, bf16[2,2304,896]{2,0,1:T(2,128)(2,1)}) async-done(((bf16[2,896,2304]{2,0,1:T(2,128)(2,1)}, bf16[2,896,2304]{2,0,1:T(2,128)(2,1)}, bf16[2,2304,896]{2,0,1:T(2,128)(2,1)}), (bf16[2,896,2304]{2,0,1:T(2,128)(2,1)}, bf16[2,896,2304]{2,0,1:T(2,128)(2,1)}, ...) | async-done | bytes 24772624
  512.6 1.9 fusion.13
  514.5 0.0 all-gather.6.cloned.1.call-update
  514.5 0.0 all-gather.4.cloned.1.call-start
  514.6 1.9 fusion.12
  516.4 0.0 all-gather.4.cloned.1.call-update
  516.5 0.0 all-gather.8.cloned.1.call-start
  517.2 0.9 constant_dynamic-slice_fusion
  518.1 1.9 fusion.14
  520.0 0.0 all-gather.8.cloned.1.call-update
  520.0 119.4 %all-gather.6.cloned.1.call-done = bf16[2,896,2304]{2,0,1:T(2,128)(2,1)} async-done(((bf16[2,7,2304]{2,0,1:T(2,128)(2,1)}), bf16[2,896,2304]{2,0,1:T(2,128)(2,1)}) %all-gather.6.cloned.1.call-update) | async-done | bytes 8257552 | tf_op jit(solution)/shard_map/all_gather | solution.py:21
  639.4 7.7 copy.37
  647.2 117.0 %all-gather.4.cloned.1.call-done = bf16[2,896,2304]{2,0,1:T(2,128)(2,1)} async-done(((bf16[2,7,2304]{2,0,1:T(2,128)(2,1)}), bf16[2,896,2304]{2,0,1:T(2,128)(2,1)}) %all-gather.4.cloned.1.call-update) | async-done | bytes 8257552 | tf_op jit(solution)/shard_map/all_gather | solution.py:21
  764.2 7.7 copy.36
  771.9 116.3 %all-gather.8.cloned.1.call-done = bf16[2,2304,896]{2,0,1:T(2,128)(2,1)} async-done(((bf16[2,18,896]{2,0,1:T(2,128)(2,1)}), bf16[2,2304,896]{2,0,1:T(2,128)(2,1)}) %all-gather.8.cloned.1.call-update) | async-done | bytes 8257552 | tf_op jit(solution)/shard_map/all_gather | solution.py:21
  888.2 7.7 copy.38
  (17 shorter events, 0.0 us)
Async XLA Ops:
  7.2 505.4 %all-reduce.6.cloned.1.call-start = ((), (), s32[]{:S(2)}) async-start(), calls=%async_computation.3 | async-start | bytes 49545216
  7.2 36.8 %copy-start = (bf16[1,2,896,2304]{3,2,1,0:T(8,128)(2,1)S(1)}, bf16[1,2,896,2304]{3,2,1,0:T(8,128)(2,1)}, u32[]{:S(2)}) copy-start(bf16[1,2,896,2304]{3,2,1,0:T(8,128)(2,1)} %param.13) | copy-start | bytes 24772612
  7.2 36.7 %copy-start.1 = (bf16[1,2,896,2304]{3,2,1,0:T(8,128)(2,1)S(1)}, bf16[1,2,896,2304]{3,2,1,0:T(8,128)(2,1)}, u32[]{:S(2)}) copy-start(bf16[1,2,896,2304]{3,2,1,0:T(8,128)(2,1)} %param.12) | copy-start | bytes 24772612
  85.9 0.7 copy-start.8
  85.9 426.6 %copy-start.2 = (f32[2,7,2304]{2,0,1:T(2,128)S(1)}, f32[2,7,2304]{2,0,1:T(2,128)}, u32[]{:S(2)}) copy-start(f32[2,7,2304]{2,0,1:T(2,128)} %param.22) | copy-start | bytes 387076
  85.9 426.6 %copy-start.3 = (f32[2,7,2304]{2,0,1:T(2,128)S(1)}, f32[2,7,2304]{2,0,1:T(2,128)}, u32[]{:S(2)}) copy-start(f32[2,7,2304]{2,0,1:T(2,128)} %param.19) | copy-start | bytes 387076
  86.0 428.6 %copy-start.4 = (f32[2,7,2304]{2,0,1:T(2,128)S(1)}, f32[2,7,2304]{2,0,1:T(2,128)}, u32[]{:S(2)}) copy-start(f32[2,7,2304]{2,0,1:T(2,128)} %param.21) | copy-start | bytes 387076
  86.0 428.6 %copy-start.5 = (f32[2,7,2304]{2,0,1:T(2,128)S(1)}, f32[2,7,2304]{2,0,1:T(2,128)}, u32[]{:S(2)}) copy-start(f32[2,7,2304]{2,0,1:T(2,128)} %param.18) | copy-start | bytes 387076
  86.0 432.1 %copy-start.6 = (f32[2,18,896]{2,0,1:T(2,128)S(1)}, f32[2,18,896]{2,0,1:T(2,128)}, u32[]{:S(2)}) copy-start(f32[2,18,896]{2,0,1:T(2,128)} %param.23) | copy-start | bytes 387076
  86.0 432.1 %copy-start.7 = (f32[2,18,896]{2,0,1:T(2,128)S(1)}, f32[2,18,896]{2,0,1:T(2,128)}, u32[]{:S(2)}) copy-start(f32[2,18,896]{2,0,1:T(2,128)} %param.20) | copy-start | bytes 387076
  86.0 553.4 %all-gather.6.cloned.1.call-start = ((), (), s32[]{:S(2)}) async-start(), calls=%async_computation.1 | async-start | bytes 8322048 | tf_op jit(solution)/shard_map/all_gather | solution.py:21
  514.5 249.7 %all-gather.4.cloned.1.call-start = ((), (), s32[]{:S(2)}) async-start(), calls=%async_computation | async-start | bytes 8322048 | tf_op jit(solution)/shard_map/all_gather | solution.py:21
  516.5 371.8 %all-gather.8.cloned.1.call-start = ((), (), s32[]{:S(2)}) async-start(), calls=%async_computation.2 | async-start | bytes 8322048 | tf_op jit(solution)/shard_map/all_gather | solution.py:21
Sparse Core Ops, SparseCore 0:
  86.2 426.3 all-reduce.5
  516.7 122.6 all-gather.5
  643.6 120.5 all-gather.3
  767.6 120.5 all-gather.7
where the time goes:
time: 904 us; the launch traced here: 902 us
  waiting for transfers between devices  776 us (86%)
  local copies, waits for them, and re-layouts  105 us (12%)
  between operations  15.2 us (2%)
    unnamed x5, waiting for transfers between devices  424 us
    all_gather x3, waiting for transfers between devices, step(): whole = [lax.all_gather(one[0], 'dp', axis=1, tiled=True) for one in new]  353 us
    unnamed x23, local copies, waits for them, and re-layouts  61.1 us
    squeeze x1, local copies, waits for them, and re-layouts, step(): t[0]  41.9 us
  transfers between devices with their start and end apart: 4, of which 4 were waited for; matrix products, arithmetic and copies ran while one was open for 2% of the time, Pallas kernels for 0%

commit v1 on v0

v1 whole, which is shorter than its diff:
```python
import math

import jax
import jax.numpy as jnp
from jax import lax
from jax.experimental import pallas as pl
from jax.experimental.pallas import tpu as pltpu
from jax.sharding import PartitionSpec as P

BF, F32 = jnp.bfloat16, jnp.float32
MESH = pl.DeviceIdType.MESH
NX, NY, NZ = 4, 4, 8
LAYERS = 2
UP_ROWS, UP_COLS = 56, 2304
DOWN_ROWS, DOWN_COLS = 144, 896
CUT = 256
SIDE = NZ * CUT
WIDE = UP_COLS + CUT
OWN_UP, OWN_DOWN = 7, 18
TILE_UP, TILE_DOWN = 8, 24


class Place:
    def __init__(self):
        me = lax.axis_index("dp")
        self.me = me
        self.x, self.y, self.z = lax.div(me, NY * NZ), lax.rem(lax.div(me, NZ), NY), lax.rem(me, NZ)

    def at_x(self, by):
        return (lax.rem(self.x + by + NX, NX) * NY + self.y) * NZ + self.z

    def at_y(self, by):
        return (self.x * NY + lax.rem(self.y + by + NY, NY)) * NZ + self.z

    def at_z(self, by):
        return (self.x * NY + self.y) * NZ + lax.rem(self.z + by + NZ, NZ)


def greet(place):
    barrier = pltpu.get_barrier_semaphore()
    peers = [place.at_x(1), place.at_x(-1)] + [place.at_y(j) for j in range(1, NY)] + [place.at_z(j) for j in range(1, NZ)]
    for peer in peers:
        pl.semaphore_signal(barrier, inc=1, device_id={"dp": peer}, device_id_type=MESH)
    pl.semaphore_wait(barrier, len(peers))


class Plan:
    def __init__(self):
        self.steps, self.started = [], []

    def add(self, when, step):
        self.steps.append((when, len(self.steps), step))

    def send(self, copy):
        copy.start()
        self.started.append(copy)

    def run(self):
        for _, _, step in sorted(self.steps, key=lambda s: s[:2]):
            step()
        for copy in self.started:
            copy.wait_send()


def remote(src, dst, send_sem, recv_sem, dev):
    return pltpu.make_async_remote_copy(src_ref=src, dst_ref=dst, send_sem=send_sem, recv_sem=recv_sem, device_id={"dp": dev}, device_id_type=MESH)


def over(shape, block, body):
    *lead, rows, _ = shape
    each = rows // block

    def one(i, _):
        row, rest, index = lax.rem(i, each), lax.div(i, each), []
        for size in reversed(lead):
            index.insert(0, lax.rem(rest, size))
            rest = lax.div(rest, size)
        body((*index, pl.ds(pl.multiple_of(row * block, block), block)))
        return 0

    lax.fori_loop(0, math.prod(lead) * each, one, 0)


def add_to(dst, parts, block):
    def body(index):
        total = parts[0][(*index, slice(None))].astype(F32)
        for part in parts[1:]:
            total = total + part[(*index, slice(None))].astype(F32)
        dst[(*index, slice(None))] = total.astype(dst.dtype)

    over(dst.shape, block, body)


class Ring:
    def __init__(self, plan, n, pos, peer, pieces, start, slot, send_sem, recv_sem, finish):
        self.plan, self.n, self.pos, self.peer, self.pieces = plan, n, pos, peer, pieces
        self.send_sem, self.recv_sem = send_sem, recv_sem
        plan.add(start, self.first)
        for m in range(n - 1):
            due = start + (m + 1) * slot + 2.5
            if m + 2 <= n - 2:
                plan.add(due, lambda m=m: self.forward(m))
        last = start + (n - 1) * slot + 2.5
        plan.add(last, lambda: self.arrive(n - 3))
        plan.add(last, lambda: self.arrive(n - 2))
        plan.add(last, finish)
        self.end = last

    def what(self, way, m):
        k = self.n // 2 - (m + 1) // 2
        layer = m % 2 if way == 0 else 1 - m % 2
        return layer, lax.rem(self.pos + (k if way == 0 else -k) + self.n, self.n)

    def copy(self, way, m, p, source):
        piece = self.pieces[p]
        return remote(source, piece["recv"](way, m), self.send_sem.at[way, m, p], self.recv_sem.at[way, m, p], self.peer(1 if way == 0 else -1))

    def first(self):
        for m in (0, 1):
            for way in (0, 1):
                for p, piece in enumerate(self.pieces):
                    self.plan.send(self.copy(way, m, p, piece["raw"](*self.what(way, m))))

    def arrive(self, m):
        for way in (0, 1):
            for p, piece in enumerate(self.pieces):
                self.copy(way, m, p, piece["recv"](way, m)).wait_recv()

    def forward(self, m):
        for way in (0, 1):
            layer, chunk = self.what(way, m + 2)
            for p, piece in enumerate(self.pieces):
                self.copy(way, m, p, piece["recv"](way, m)).wait_recv()
                own = piece["own"](way, m + 2, layer, chunk)
                add_to(own, [own, piece["recv"](way, m)], piece["block"])
                self.plan.send(self.copy(way, m + 2, p, own))

    def parts(self, p, layer):
        piece, n = self.pieces[p], self.n
        right, left = (n - 2, n - 3) if layer == 0 else (n - 3, n - 2)
        return [piece["mine"](layer), piece["recv"](0, right), piece["recv"](1, left)]


def scatter_kernel(gate, up, down, g0, g1, g2, *scratch):
    (a0_own, a0_recv, b0_recv, t0, c0_recv, f0, a1_own, a1_recv, b1_recv, t1, c1_recv, f1, a2_own, a2_recv, b2_recv, d2_recv, t2, f2) = scratch[:18]
    (local, sa0, ra0, sb0, rb0, sc0, rc0, sa1, ra1, sb1, rb1, sc1, rc1, sa2, ra2, sb2, rb2, sd2, rd2, se2, re2) = scratch[18:]
    place = Place()
    x, y, z = place.x, place.y, place.z
    plan = Plan()
    loads = {}

    def load(name, copies):
        loads[name] = copies
        for copy in copies:
            copy.start()

    def ready(name):
        for copy in loads.pop(name):
            copy.wait()

    def slot(n, way, m):
        return 2 + way * (n - 3) + m - 2

    pieces_a0 = [dict(
        raw=lambda l, c: down.at[l, c],
        own=lambda way, m, l, c: a0_own.at[slot(NX, way, m)],
        mine=lambda l: a0_own.at[l],
        recv=lambda way, m: a0_recv.at[way, m],
        block=16,
    )]
    pieces_a1 = [
        dict(
            raw=lambda l, c: up.at[l, :, c],
            own=lambda way, m, l, c: a1_own.at[slot(NY, way, m), :, :, pl.ds(0, UP_COLS)],
            mine=lambda l: a1_own.at[l, :, :, pl.ds(0, UP_COLS)],
            recv=lambda way, m: a1_recv.at[way, m, :, :, pl.ds(0, UP_COLS)],
            block=8,
        ),
        dict(
            raw=lambda l, c: gate.at[l, :, c, :, pl.ds(SIDE, CUT)],
            own=lambda way, m, l, c: a1_own.at[slot(NY, way, m), :, :, pl.ds(UP_COLS, CUT)],
            mine=lambda l: a1_own.at[l, :, :, pl.ds(UP_COLS, CUT)],
            recv=lambda way, m: a1_recv.at[way, m, :, :, pl.ds(UP_COLS, CUT)],
            block=56,
        ),
    ]
    pieces_a2 = [dict(
        raw=lambda l, c: gate.at[l, :, :, :, pl.ds(pl.multiple_of(c * CUT, CUT), CUT)],
        own=lambda way, m, l, c: a2_own.at[slot(NZ, way, m)],
        mine=lambda l: a2_own.at[l],
        recv=lambda way, m: a2_recv.at[way, m],
        block=56,
    )]

    def fetch(tag, ring, first_sem, messages):
        copies, sem = [], first_sem
        for m in messages:
            for way in (0, 1):
                for piece in ring.pieces:
                    if m is None:
                        src, dst = piece["raw"](way, ring.pos), piece["mine"](way)
                    else:
                        layer, chunk = ring.what(way, m)
                        src, dst = piece["raw"](layer, chunk), piece["own"](way, m, layer, chunk)
                    copies.append(pltpu.make_async_copy(src, dst, local.at[sem]))
                    sem += 1
        load(tag, copies)
        return sem

    def finish_a0():
        ready("mine0")
        for l in range(LAYERS):
            add_to(ring_a0.pieces[0]["mine"](l), ring_a0.parts(0, l), 16)

    def finish_b0():
        for l in range(LAYERS):
            own, right, left = ring_b0.parts(0, l)
            add_to(f0.at[pl.ds(0, DOWN_ROWS)], [own, right, left], 16)
            for c in range(NZ):
                t0[c, l] = f0[pl.ds(c * OWN_DOWN, TILE_DOWN), :].astype(BF)

    def finish_c0():
        for l in range(LAYERS):
            add_to(g0.at[l], ring_c0.parts(0, l), TILE_DOWN)

    ring_a0 = Ring(plan, NX, x, place.at_x, pieces_a0, 0.0, 22.1, sa0, ra0, finish_a0)
    ring_b0 = Ring(plan, NY, y, place.at_y, [dict(
        raw=lambda l, c: a0_own.at[l, c],
        own=lambda way, m, l, c: a0_own.at[l, c],
        mine=lambda l: a0_own.at[l, y],
        recv=lambda way, m: b0_recv.at[way, m],
        block=16,
    )], ring_a0.end + 0.1, 5.6, sb0, rb0, finish_b0)
    ring_c0 = Ring(plan, NZ, z, place.at_z, [dict(
        raw=lambda l, c: t0.at[c, l],
        own=lambda way, m, l, c: t0.at[c, l],
        mine=lambda l: t0.at[z, l],
        recv=lambda way, m: c0_recv.at[way, m],
        block=TILE_DOWN,
    )], ring_b0.end + 0.1, 1.7, sc0, rc0, finish_c0)

    def finish_a1():
        ready("mine1")
        for l in range(LAYERS):
            for p in (0, 1):
                add_to(ring_a1.pieces[p]["mine"](l), ring_a1.parts(p, l), ring_a1.pieces[p]["block"])

    def finish_b1():
        for l in range(LAYERS):
            own, right, left = ring_b1.parts(0, l)
            add_to(f1.at[pl.ds(0, UP_ROWS)], [own, right, left], 8)
            for c in range(NZ):
                t1[c, l] = f1[pl.ds(c * OWN_UP, TILE_UP), :].astype(BF)

    def finish_c1():
        for l in range(LAYERS):
            add_to(g1.at[l], ring_c1.parts(0, l), TILE_UP)

    ring_a1 = Ring(plan, NY, y, place.at_y, pieces_a1, 0.01, 24.6, sa1, ra1, finish_a1)
    ring_b1 = Ring(plan, NX, x, place.at_x, [dict(
        raw=lambda l, c: a1_own.at[l, c],
        own=lambda way, m, l, c: a1_own.at[l, c],
        mine=lambda l: a1_own.at[l, x],
        recv=lambda way, m: b1_recv.at[way, m],
        block=8,
    )], ring_a1.end + 0.1, 6.2, sb1, rb1, finish_b1)
    ring_c1 = Ring(plan, NZ, z, place.at_z, [dict(
        raw=lambda l, c: t1.at[c, l],
        own=lambda way, m, l, c: t1.at[c, l],
        mine=lambda l: t1.at[z, l],
        recv=lambda way, m: c1_recv.at[way, m],
        block=TILE_UP,
    )], ring_b1.end + 0.1, 1.7, sc1, rc1, finish_c1)

    def finish_a2():
        ready("mine2")
        for l in range(LAYERS):
            add_to(ring_a2.pieces[0]["mine"](l), ring_a2.parts(0, l), 56)

    def finish_b2():
        for l in range(LAYERS):
            add_to(ring_b2.pieces[0]["mine"](l), ring_b2.parts(0, l), 56)
        for j in range(1, NY):
            plan.send(across(j))

    def across(j):
        to = lax.rem(y + j, NY)
        return remote(a2_own.at[pl.ds(0, LAYERS), x, to], d2_recv.at[j - 1], sd2.at[j - 1], rd2.at[j - 1], place.at_y(j))

    def finish_d2():
        for j in range(1, NY):
            across(j).wait_recv()
        for l in range(LAYERS):
            add_to(f2.at[pl.ds(0, UP_ROWS)], [a2_own.at[l, x, y]] + [d2_recv.at[j, l] for j in range(NY - 1)], 56)
            for c in range(NZ):
                t2[c, l] = f2[pl.ds(c * OWN_UP, TILE_UP), :].astype(BF)
        for j in range(1, NZ):
            plan.send(turn(j))
        g2[z] = t2[z]

    def turn(j):
        return remote(t2.at[lax.rem(z + j, NZ)], g2.at[z], se2.at[j - 1], re2.at[j - 1], place.at_z(j))

    def finish_e2():
        for j in range(1, NZ):
            turn(j).wait_recv()

    ring_a2 = Ring(plan, NZ, z, place.at_z, pieces_a2, 0.02, 9.85, sa2, ra2, finish_a2)
    ring_b2 = Ring(plan, NX, x, place.at_x, [dict(
        raw=lambda l, c: a2_own.at[l, c],
        own=lambda way, m, l, c: a2_own.at[l, c],
        mine=lambda l: a2_own.at[l, x],
        recv=lambda way, m: b2_recv.at[way, m],
        block=56,
    )], ring_a2.end + 0.1, 4.0, sb2, rb2, finish_b2)
    plan.add(ring_b2.end + 6.0, finish_d2)
    plan.add(max(ring_b2.end + 12.0, ring_c0.end, ring_c1.end) + 1.0, finish_e2)

    def begin():
        f0[pl.ds(DOWN_ROWS, 8), :] = jnp.zeros((8, DOWN_COLS), F32)
        f1[pl.ds(UP_ROWS, 8), :] = jnp.zeros((8, WIDE), F32)
        f2[pl.ds(UP_ROWS, 8), :] = jnp.zeros((8, CUT), F32)
        sem = 0
        for m in range(2, NZ - 1):
            sem = fetch(f"a2_{m}", ring_a2, sem, [m])
            if m == 3:
                sem = fetch("a0", ring_a0, sem, [2])
                sem = fetch("a1", ring_a1, sem, [2])
        sem = fetch("mine2", ring_a2, sem, [None])
        sem = fetch("mine0", ring_a0, sem, [None])
        sem = fetch("mine1", ring_a1, sem, [None])

    plan.add(0.5, begin)
    plan.add(1.0, lambda: ready("a0"))
    plan.add(1.0, lambda: ready("a1"))
    for m in range(2, NZ - 1):
        plan.add(1.0, lambda m=m: ready(f"a2_{m}"))

    greet(place)
    plan.run()


def adamw(w, m, v, g):
    m = 0.9 * m + 0.1 * g
    v = 0.95 * v + 0.05 * g * g
    step = m * lax.rsqrt(v + 1e-8) + 0.1 * w
    return w - 0.02 * step, m, v


def step_kernel(g0, g1, g2, w_gate, w_up, w_down, m_gate, m_up, m_down, v_gate, v_up, v_down,
                n_m_gate, n_m_up, n_m_down, n_v_gate, n_v_up, n_v_down, n0, n1, n2,
                old_gate, old_up, old_down, wide, tall, short, sems):
    place = Place()
    z, slab = place.z, place.x * NY + place.y
    tile = slab * 7 + lax.div(z * OWN_UP, 8)
    copies = []
    for i, (w, old) in enumerate(((w_gate, old_gate), (w_up, old_up))):
        copies.append(pltpu.make_async_copy(w.at[:, tile], old.at[:, 0], sems.at[2 * i]))
        copies.append(pltpu.make_async_copy(w.at[:, tile + 1 - lax.div(z, NZ - 1)], old.at[:, 1], sems.at[2 * i + 1]))
    copies.append(pltpu.make_async_copy(w_down.at[:, pl.ds(slab * 18 + lax.div(z * OWN_DOWN, 8), 3)], old_down, sems.at[4]))
    for copy in copies:
        copy.start()
    for copy in copies:
        copy.wait()
    off = lax.rem(z * OWN_UP, 8)
    short[pl.ds(OWN_UP, 1), :] = jnp.zeros((1, UP_COLS), F32)
    for l in range(LAYERS):
        for old, m, v, n_m, n_v, which in ((old_gate, m_gate, v_gate, n_m_gate, n_v_gate, 0), (old_up, m_up, v_up, n_m_up, n_v_up, 1)):
            for t in range(2):
                wide[pl.ds(t * 8, 8), :] = old[l, t].astype(F32)
            w = pltpu.roll(wide[...], lax.rem(16 - off, 16), 0)[:OWN_UP]
            if which == 0:
                g = jnp.concatenate([g2[s, l] for s in range(NZ)] + [g1[l, :, pl.ds(UP_COLS, CUT)]], axis=1)
            else:
                g = g1[l, :, pl.ds(0, UP_COLS)]
            w, new_m, new_v = adamw(w, m[l], v[l], g.astype(F32)[:OWN_UP])
            n_m[l] = new_m
            n_v[l] = new_v
            short[pl.ds(0, OWN_UP), :] = w
            out = short[...].astype(BF)
            if which == 0:
                for s in range(NZ):
                    n2[s, l] = out[:, s * CUT : (s + 1) * CUT]
                n1[l, :, pl.ds(UP_COLS, CUT)] = out[:, SIDE:]
            else:
                n1[l, :, pl.ds(0, UP_COLS)] = out
    off = lax.rem(z * OWN_DOWN, 8)
    for l in range(LAYERS):
        for t in range(3):
            tall[pl.ds(t * 8, 8), :] = old_down[l, t].astype(F32)
        w = pltpu.roll(tall[pl.ds(0, 24), :], lax.rem(24 - off, 24), 0)[:OWN_DOWN]
        w, new_m, new_v = adamw(w, m_down[l], v_down[l], g0[l].astype(F32)[:OWN_DOWN])
        n_m_down[l] = new_m
        n_v_down[l] = new_v
        tall[pl.ds(0, OWN_DOWN), :] = w
        n0[l] = tall[...].astype(BF)


class Spread:
    def __init__(self, plan, n, pos, peer, pieces, start, slot, send_sem, recv_sem, finish, own=None):
        self.plan, self.n, self.pos, self.peer, self.pieces, self.own = plan, n, pos, peer, pieces, own
        self.send_sem, self.recv_sem = send_sem, recv_sem
        plan.add(start, self.first)
        for m in range(n - 1):
            plan.add(start + (m + 1) * slot + 2.5, lambda m=m: self.forward(m))
        self.end = start + (n - 1) * slot + 2.5
        plan.add(self.end, finish)

    def copy(self, way, m, p, first=False):
        k = m // 2
        layer = m % 2 if way == 0 else 1 - m % 2
        chunk = lax.rem(self.pos + (-k if way == 0 else k) + self.n, self.n)
        ref = self.pieces[p](layer, chunk)
        source = self.own[p](layer) if first and self.own else ref
        return remote(source, ref, self.send_sem.at[way, m, p], self.recv_sem.at[way, m, p], self.peer(1 if way == 0 else -1))

    def first(self):
        for m in (0, 1):
            for way in (0, 1):
                for p in range(len(self.pieces)):
                    self.plan.send(self.copy(way, m, p, True))

    def forward(self, m):
        for way in (0, 1):
            for p in range(len(self.pieces)):
                self.copy(way, m, p).wait_recv()
                if m + 2 <= self.n - 2:
                    self.plan.send(self.copy(way, m + 2, p))


def gather_kernel(n0, n1, n2, gate, up, down, z0, z1, d2, f0, f1, f2, sz0, rz0, sy0, ry0, sx0, rx0, sz1, rz1, sx1, rx1, sy1, ry1, se2, re2, sd2, rd2, sx2, rx2, sz2, rz2):
    place = Place()
    x, y, z = place.x, place.y, place.z
    plan = Plan()
    mine = pl.ds(pl.multiple_of(z * CUT, CUT), CUT)

    def build0():
        z0[z] = n0[...]
        for l in range(LAYERS):
            for c in range(NZ):
                f0[pl.ds(c * OWN_DOWN, OWN_DOWN), :] = z0[c, l].astype(F32)[:OWN_DOWN]
            add_to(down.at[l, x, y], [f0], 16)

    spread_z0 = Spread(plan, NZ, z, place.at_z, [lambda l, c: z0.at[c, l]], 0.01, 1.7, sz0, rz0, build0, [lambda l: n0.at[l]])
    spread_y0 = Spread(plan, NY, y, place.at_y, [lambda l, c: down.at[l, x, c]], spread_z0.end + 0.1, 5.6, sy0, ry0, lambda: None)
    Spread(plan, NX, x, place.at_x, [lambda l, c: down.at[l, c]], spread_y0.end + 0.1, 22.1, sx0, rx0, lambda: None)

    def build1():
        z1[z] = n1[...]
        for l in range(LAYERS):
            for c in range(NZ):
                f1[pl.ds(c * OWN_UP, OWN_UP), :] = z1[c, l].astype(F32)[:OWN_UP]
            add_to(up.at[l, x, y], [f1.at[:, pl.ds(0, UP_COLS)]], 8)
            add_to(gate.at[l, x, y, :, pl.ds(SIDE, CUT)], [f1.at[:, pl.ds(UP_COLS, CUT)]], 8)

    spread_z1 = Spread(plan, NZ, z, place.at_z, [lambda l, c: z1.at[c, l]], 0.02, 1.7, sz1, rz1, build1, [lambda l: n1.at[l]])
    spread_x1 = Spread(plan, NX, x, place.at_x, [lambda l, c: up.at[l, c, y], lambda l, c: gate.at[l, c, y, :, pl.ds(SIDE, CUT)]], spread_z1.end + 0.1, 6.2, sx1, rx1, lambda: None)
    Spread(plan, NY, y, place.at_y, [lambda l, c: up.at[l, :, c], lambda l, c: gate.at[l, :, c, :, pl.ds(SIDE, CUT)]], spread_x1.end + 0.1, 24.6, sy1, ry1, lambda: None)

    def turn(j):
        return remote(n2.at[lax.rem(z + j, NZ)], d2.at[z], se2.at[j - 1], re2.at[j - 1], place.at_z(j))

    def begin2():
        for j in range(1, NZ):
            plan.send(turn(j))
        d2[z] = n2[z]

    def across(j):
        here = gate.at[:, x, y, :, mine]
        return remote(here, here, sd2.at[j - 1], rd2.at[j - 1], place.at_y(j))

    def build2():
        for j in range(1, NZ):
            turn(j).wait_recv()
        for l in range(LAYERS):
            for c in range(NZ):
                f2[pl.ds(c * OWN_UP, OWN_UP), :] = d2[c, l].astype(F32)[:OWN_UP]
            add_to(gate.at[l, x, y, :, mine], [f2], 56)
        for j in range(1, NY):
            plan.send(across(j))

    def across_done():
        for j in range(1, NY):
            across(j).wait_recv()

    plan.add(0.0, begin2)
    plan.add(6.0, build2)
    plan.add(12.0, across_done)
    spread_x2 = Spread(plan, NX, x, place.at_x, [lambda l, c: gate.at[l, c, :, :, mine]], 12.1, 4.0, sx2, rx2, lambda: None)
    Spread(plan, NZ, z, place.at_z, [lambda l, c: gate.at[l, :, :, :, pl.ds(pl.multiple_of(c * CUT, CUT), CUT)]], spread_x2.end + 0.1, 9.85, sz2, rz2, lambda: None)

    greet(place)
    plan.run()


def out_kernel(*refs):
    sources, results, sems = refs[:3], refs[3:6], refs[6]
    copies = [pltpu.make_async_copy(a.at[l, i], b.at[l, i], sems.at[w, l, i]) for w, (a, b) in enumerate(zip(sources, results)) for l in range(LAYERS) for i in range(NX)]
    for copy in copies:
        copy.start()
    for copy in copies:
        copy.wait()


def ring_sems(n, pieces=1):
    return [pltpu.SemaphoreType.DMA((2, n - 1, pieces))] * 2


def solution(mesh):
    anywhere, vmem = pl.BlockSpec(memory_space=pltpu.HBM), pl.BlockSpec(memory_space=pltpu.VMEM)

    def body(*arrays):
        gate, up, down = (t.reshape(LAYERS, NX, NY, rows, cols) for t, rows, cols in zip(arrays[:3], (UP_ROWS, UP_ROWS, DOWN_ROWS), (UP_COLS, UP_COLS, DOWN_COLS)))
        g0, g1, g2 = pl.pallas_call(
            scatter_kernel,
            name="scatter",
            out_shape=[jax.ShapeDtypeStruct((LAYERS, TILE_DOWN, DOWN_COLS), BF), jax.ShapeDtypeStruct((LAYERS, TILE_UP, WIDE), BF), jax.ShapeDtypeStruct((NZ, LAYERS, TILE_UP, CUT), BF)],
            in_specs=[anywhere] * 3,
            out_specs=[vmem] * 3,
            scratch_shapes=[
                pltpu.VMEM((2 + 2 * (NX - 3), NY, DOWN_ROWS, DOWN_COLS), BF),
                pltpu.VMEM((2, NX - 1, NY, DOWN_ROWS, DOWN_COLS), BF),
                pltpu.VMEM((2, NY - 1, DOWN_ROWS, DOWN_COLS), BF),
                pltpu.VMEM((NZ, LAYERS, TILE_DOWN, DOWN_COLS), BF),
                pltpu.VMEM((2, NZ - 1, TILE_DOWN, DOWN_COLS), BF),
                pltpu.VMEM((DOWN_ROWS + 8, DOWN_COLS), F32),
                pltpu.VMEM((2 + 2 * (NY - 3), NX, UP_ROWS, WIDE), BF),
                pltpu.VMEM((2, NY - 1, NX, UP_ROWS, WIDE), BF),
                pltpu.VMEM((2, NX - 1, UP_ROWS, WIDE), BF),
                pltpu.VMEM((NZ, LAYERS, TILE_UP, WIDE), BF),
                pltpu.VMEM((2, NZ - 1, TILE_UP, WIDE), BF),
                pltpu.VMEM((UP_ROWS + 8, WIDE), F32),
                pltpu.VMEM((2 + 2 * (NZ - 3), NX, NY, UP_ROWS, CUT), BF),
                pltpu.VMEM((2, NZ - 1, NX, NY, UP_ROWS, CUT), BF),
                pltpu.VMEM((2, NX - 1, NY, UP_ROWS, CUT), BF),
                pltpu.VMEM((NY - 1, LAYERS, UP_ROWS, CUT), BF),
                pltpu.VMEM((NZ, LAYERS, TILE_UP, CUT), BF),
                pltpu.VMEM((UP_ROWS + 8, CUT), F32),
                pltpu.SemaphoreType.DMA((2 * (NZ - 3) + 2 + 4 + 8,)),
                *ring_sems(NX), *ring_sems(NY), *ring_sems(NZ),
                *ring_sems(NY, 2), *ring_sems(NX), *ring_sems(NZ),
                *ring_sems(NZ), *ring_sems(NX),
                *[pltpu.SemaphoreType.DMA((NY - 1,))] * 2,
                *[pltpu.SemaphoreType.DMA((NZ - 1,))] * 2,
            ],
            compiler_params=pltpu.CompilerParams(collective_id=0, has_side_effects=True, vmem_limit_bytes=60 * 2**20),
        )(gate, up, down)

        w_gate, w_up, w_down = (w.reshape(LAYERS, -1, 8, w.shape[-1]) for w in arrays[3:6])
        moments = arrays[6:12]
        *new, n0, n1, n2 = pl.pallas_call(
            step_kernel,
            name="step",
            out_shape=[jax.ShapeDtypeStruct(a.shape, F32) for a in moments] + [jax.ShapeDtypeStruct(a.shape, BF) for a in (g0, g1, g2)],
            in_specs=[vmem] * 3 + [anywhere] * 3 + [vmem] * 6,
            out_specs=[vmem] * 9,
            scratch_shapes=[
                pltpu.VMEM((LAYERS, 2, 8, UP_COLS), BF),
                pltpu.VMEM((LAYERS, 2, 8, UP_COLS), BF),
                pltpu.VMEM((LAYERS, 3, 8, DOWN_COLS), BF),
                pltpu.VMEM((16, UP_COLS), F32),
                pltpu.VMEM((TILE_DOWN, DOWN_COLS), F32),
                pltpu.VMEM((8, UP_COLS), F32),
                pltpu.SemaphoreType.DMA((5,)),
            ],
            compiler_params=pltpu.CompilerParams(vmem_limit_bytes=20 * 2**20),
        )(g0, g1, g2, w_gate, w_up, w_down, *moments)

        whole = pl.pallas_call(
            gather_kernel,
            name="gather",
            out_shape=[pltpu.VMEM(a.shape, BF) for a in (gate, up, down)],
            in_specs=[vmem] * 3,
            out_specs=[vmem] * 3,
            scratch_shapes=[
                pltpu.VMEM((NZ, LAYERS, TILE_DOWN, DOWN_COLS), BF),
                pltpu.VMEM((NZ, LAYERS, TILE_UP, WIDE), BF),
                pltpu.VMEM((NZ, LAYERS, TILE_UP, CUT), BF),
                pltpu.VMEM((DOWN_ROWS, DOWN_COLS), F32),
                pltpu.VMEM((UP_ROWS, WIDE), F32),
                pltpu.VMEM((UP_ROWS, CUT), F32),
                *ring_sems(NZ), *ring_sems(NY), *ring_sems(NX),
                *ring_sems(NZ), *ring_sems(NX, 2), *ring_sems(NY, 2),
                *[pltpu.SemaphoreType.DMA((NZ - 1,))] * 2,
                *[pltpu.SemaphoreType.DMA((NY - 1,))] * 2,
                *ring_sems(NX), *ring_sems(NZ),
            ],
            compiler_params=pltpu.CompilerParams(collective_id=1, has_side_effects=True, vmem_limit_bytes=16 * 2**20),
        )(n0, n1, n2)
        whole = pl.pallas_call(
            out_kernel,
            name="out",
            out_shape=[jax.ShapeDtypeStruct(a.shape, BF) for a in (gate, up, down)],
            in_specs=[vmem] * 3,
            out_specs=[anywhere] * 3,
            scratch_shapes=[pltpu.SemaphoreType.DMA((3, LAYERS, NX))],
            compiler_params=pltpu.CompilerParams(vmem_limit_bytes=2 * 2**20),
        )(*whole)
        whole = [w.reshape(LAYERS, -1, w.shape[-1]) for w in whole]
        return (*whole, *new)

    all_of, cut = P(None, None, None), P(None, "dp", None)
    return jax.shard_map(
        body,
        mesh=mesh,
        in_specs=(P(("rep", "dp"), None, None, None),) * 3 + (all_of,) * 3 + (cut,) * 6,
        out_specs=(P("rep", None, None),) * 3 + (P("rep", "dp", None),) * 6,
        check_vma=False,
    )
```

time: 904 us -> 270 us (0.30)
  waiting for transfers between devices: 776 us -> 0 us
  Pallas kernels: 0 us -> 246 us
  local copies, waits for them, and re-layouts: 105 us -> 22.5 us
  between operations: 15.2 us -> 0.7 us
    unnamed x5 -> x0, waiting for transfers between devices: 424 us -> none
    all_gather x3 -> x0, waiting for transfers between devices: 353 us -> none  [step(): whole = [lax.all_gather(one[0], 'dp', axis=1, tiled=True) for one in new]]
    pallas_call x0 -> x4, Pallas kernels: none -> 246 us  [the longest x1 132 us: body(): pl.pallas_call(scatter_kernel, name='scatter', out_shape=[jax.ShapeDtypeS...]
    squeeze x1 -> x0, local copies, waits for them, and re-layouts: 41.9 us -> none  [step(): t[0]]
    unnamed x23 -> x24, local copies, waits for them, and re-layouts: 61.1 us -> 22.5 us
  transfers between devices with their start and end apart: 4 -> 0, of which waited for: 4 -> 0; matrix products, arithmetic and copies ran while one was open for 2% -> 0% of each run, Pallas kernels for 0% -> 0%
where the time goes in v1:
time: 270 us; the launch traced here: 269 us
  Pallas kernels  246 us (91%)
  local copies, waits for them, and re-layouts  22.5 us (8%)
    pallas_call x1, Pallas kernels, body(): pl.pallas_call(scatter_kernel, name='scatter', out_shape=[jax.ShapeDtypeS...  132 us
    pallas_call x1, Pallas kernels, body(): pl.pallas_call(gather_kernel, name='gather', out_shape=[pltpu.VMEM(a.shap...  105 us
    unnamed x24, local copies, waits for them, and re-layouts  22.5 us
    pallas_call x1, Pallas kernels, body(): pl.pallas_call(out_kernel, name='out', out_shape=[jax.ShapeDtypeStruct(a....  8.46 us

profile of v1, /device:TPU:32, one launch (start us, length us, event | category | flops | bytes accessed | tf_op | source)
XLA Modules:
  0.0 269.4 jit_solution(3378302836221461033)
XLA Ops:
  0.6 0.9 copy.21.m_gate
  1.6 0.9 copy.22.m_up
  2.5 0.9 copy.24.v_gate
  3.4 0.9 copy.25.v_up
  4.4 0.9 copy.23.m_down
  5.3 0.9 copy.26.v_down
  6.2 131.9 %scatter.1 = (bf16[2,24,896]{2,1,0:T(8,128)(2,1)}, bf16[2,8,2560]{2,1,0:T(8,128)(2,1)}, bf16[8,2,8,256]{3,2,1,0:T(8,128)(2,1)}) custom-call(bf16[2,4,4,56,2304]{4,3,2,1,0:T(8,128)(2,1)} %bitcast.12, bf16[2,4,4,56,2304]{4,3,2,1,0:T(8,128)(2,1)} %bitcast.13, bf16[2,4,4,144,896]{4,3,2,1,0:T(8,128)(2,1)} %bitcast.14), custom_call_target="tpu_custom_call" | custom-call | tf_op jit(solution)/shard_map/scatter/pallas_call | solution.py:514
  138.1 0.0 copy-start
  138.2 3.3 %copy-done = bf16[2,896,2304]{2,1,0:T(8,128)(2,1)S(1)} copy-done((bf16[2,896,2304]{2,1,0:T(8,128)(2,1)S(1)}, bf16[2,896,2304]{2,1,0:T(8,128)(2,1)}, u32[]{:S(2)}) %copy-start) | copy-done | bytes 8257560
  141.5 0.0 copy-start.1
  141.5 3.3 %copy-done.1 = bf16[2,896,2304]{2,1,0:T(8,128)(2,1)S(1)} copy-done((bf16[2,896,2304]{2,1,0:T(8,128)(2,1)S(1)}, bf16[2,896,2304]{2,1,0:T(8,128)(2,1)}, u32[]{:S(2)}) %copy-start.1) | copy-done | bytes 8257560
  144.8 3.3 %copy-done.2 = bf16[2,2304,896]{2,1,0:T(8,128)(2,1)S(1)} copy-done((bf16[2,2304,896]{2,1,0:T(8,128)(2,1)S(1)}, bf16[2,2304,896]{2,1,0:T(8,128)(2,1)}, u32[]{:S(2)}) %copy-start.2) | copy-done | bytes 8257560
  148.2 0.9 copy-done.3
  149.1 0.9 copy-done.4
  150.0 0.8 copy-done.5
  150.8 0.7 step.1
  151.5 0.7 copy.27
  152.2 0.7 copy.28
  152.9 0.7 copy.29
  153.7 0.7 copy.30
  154.4 0.7 copy.31
  155.1 0.7 copy.32
  155.8 105.1 %gather.1 = (bf16[2,4,4,56,2304]{4,3,2,1,0:T(8,128)(2,1)S(1)}, bf16[2,4,4,56,2304]{4,3,2,1,0:T(8,128)(2,1)S(1)}, bf16[2,4,4,144,896]{4,3,2,1,0:T(8,128)(2,1)S(1)}) custom-call(bf16[2,24,896]{2,1,0:T(8,128)(2,1)S(1)} %get-tuple-element.30.n0, bf16[2,8,2560]{2,1,0:T(8,128)(2,1)S(1)} %get-tuple-element.31.n1, bf16[8,2,8,256]{3,2,1,0:T(8,128)(2,1)S(1)} %get-tuple-element.32.n2), custom_call_target="tpu_custom_call" | custom-call | tf_op jit(solution)/shard_map/gather/pallas_call | solution.py:569
  260.9 8.5 %out.1 = (bf16[2,4,4,56,2304]{4,3,2,1,0:T(8,128)(2,1)}, bf16[2,4,4,56,2304]{4,3,2,1,0:T(8,128)(2,1)}, bf16[2,4,4,144,896]{4,3,2,1,0:T(8,128)(2,1)}) custom-call(bf16[2,4,4,56,2304]{4,3,2,1,0:T(8,128)(2,1)S(1)} %get-tuple-element.33.refs_0_, bf16[2,4,4,56,2304]{4,3,2,1,0:T(8,128)(2,1)S(1)} %get-tuple-element.34.refs_1_, ...), custom_call_target="tpu_custom_call" | custom-call | tf_op jit(solution)/shard_map/out/pallas_call | solution.py:590
  (4 shorter events, 0.0 us)
Async XLA Ops:
  138.1 3.3 %copy-start = (bf16[2,896,2304]{2,1,0:T(8,128)(2,1)S(1)}, bf16[2,896,2304]{2,1,0:T(8,128)(2,1)}, u32[]{:S(2)}) copy-start(bf16[2,896,2304]{2,1,0:T(8,128)(2,1)} %param.15) | copy-start | bytes 24772612
  141.5 3.3 %copy-start.1 = (bf16[2,896,2304]{2,1,0:T(8,128)(2,1)S(1)}, bf16[2,896,2304]{2,1,0:T(8,128)(2,1)}, u32[]{:S(2)}) copy-start(bf16[2,896,2304]{2,1,0:T(8,128)(2,1)} %param.16) | copy-start | bytes 24772612
  144.8 3.3 %copy-start.2 = (bf16[2,2304,896]{2,1,0:T(8,128)(2,1)S(1)}, bf16[2,2304,896]{2,1,0:T(8,128)(2,1)}, u32[]{:S(2)}) copy-start(bf16[2,2304,896]{2,1,0:T(8,128)(2,1)} %param.17) | copy-start | bytes 24772612
  148.2 0.9 copy-start.3
  149.1 0.9 copy-start.4
  150.0 0.8 copy-start.5
